TPU v7x, 256 devices: a whole 4x4x8 slice. The times are simulated.
256 devices in a mesh: section: 32 (over y, x, z_lo), tensor: 8 (over z_hi, core).
Axes of the slice: x: 4, y: 4, z: 8 (z_hi: 4, z_lo: 2; z = z_hi * 2 + z_lo), core: 2. Of those that a mesh axis runs over, the one named last changes fastest.
Arguments:
- hidden_in: bfloat16 [128, 8192], P(None, 'tensor'), may hold values from -36 to 36
- segment_ids: int32 [4, 32], replicated, may hold values from 0 to 7, never falling along the last dimension, each value on 1 to 8 neighbouring positions
- segment_job: int32 [4, 8], replicated, may hold values from 0 to 5
- job_adapter: int32 [6], replicated, may hold values from 0 to 3
- owner: int32 [32], P('section'), may hold values from 0 to 7
- frozen: bfloat16 [32, 8192, 4096], P('section', None, 'tensor'), may hold values from -0.0625 to 0.0625
- norm_gain: bfloat16 [32, 4096], P('section'), may hold values from 0.3984375 to 1.59375
- inbox_down: bfloat16 [32, 8, 4096, 128], P('section', 'tensor'), may hold values from -0.0625 to 0.0625
- inbox_up: bfloat16 [32, 8, 128, 4096], P('section', 'tensor'), may hold values from -1 to 1
Outputs:
- section_out: bfloat16 [32, 128, 4096], P('section', None, 'tensor')
Inputs may be any that keep to these rules, and one draw needn't show every extreme that they name: `segment_ids`: within each micro-batch the segment numbers never fall, and each of the 8 segments has 1 to 8 tokens.
All inputs are finite; a program needn't handle non-finite values.
Results may differ from a plain program's by a relative error of at most 0.02.
Values may be sent and summed in bfloat16 or wider, within the bound.
No kernel may reach another device: no remote copies, remote signals or barrier semaphores. Data moves between devices by JAX's collectives and lax.ppermute only.
A program may use at most 64 MiB of HBM per device.

v0:
```python
import jax
import jax.numpy as jnp
from jax import lax
from jax.sharding import PartitionSpec as P

R = 32
epsilon = 1e-05


def spread(block, axis, owner):
    block = jnp.where(lax.axis_index(axis) == owner, block, jnp.zeros_like(block))
    return lax.psum(block, axis)


def from_partner(value, axis, bit):
    mask = 2**bit
    pairs = [(source, source ^ mask) for source in range(lax.axis_size(axis))]
    return lax.ppermute(value, axis, pairs)


def side_by_side(arrays, axis, dim, along):
    ends, at = ([], 0)
    for a in arrays[:-1]:
        at += a.shape[along]
        ends.append(at)
    both = jnp.concatenate(arrays, axis=along)
    return tuple(jnp.split(lax.all_gather(both, axis, axis=dim, tiled=True), ends, axis=along))


def shifted(value, axis, steps):
    count = lax.axis_size(axis)
    first, last = (max(0, -steps), min(count, count - steps))
    return lax.ppermute(value, axis, [(source, source + steps) for source in range(first, last)])


def product(left, right):
    return jnp.dot(left, right, preferred_element_type=jnp.float32)


def both_halves(own_part, other_part, pair_side):
    lower_part = jnp.where(pair_side == 0, own_part, other_part)
    upper_part = jnp.where(pair_side == 0, other_part, own_part)
    return (lower_part, upper_part)


def local(
    hidden_in, segment_ids, segment_job, job_adapter, owner, frozen, norm_gain, inbox_down, inbox_up
):
    tensors = lax.axis_size("tensor")
    sections = lax.axis_size("section")
    levels = sections // 2
    piece_cols = frozen.shape[2]
    half_width = norm_gain.shape[1]
    full_width = 2 * half_width
    rank_cols = inbox_down.shape[3]
    unit_count = segment_ids.shape[0]
    unit_rows = segment_ids.shape[1]
    position = lax.axis_index("section")
    pair_side = position % 2
    section_level = position // 2
    shard_index = lax.axis_index("tensor")
    down_half, up_half = (
        spread(inbox_down[0, 0], "tensor", owner[0]),
        spread(inbox_up[0, 0], "tensor", owner[0]),
    )
    up_own = lax.dynamic_slice_in_dim(up_half, shard_index * piece_cols, piece_cols, 1)
    split_weight = frozen[0].reshape(tensors, 2, piece_cols, piece_cols)
    weight_low = split_weight[:, 0].reshape(half_width, piece_cols)
    weight_high = split_weight[:, 1].reshape(half_width, piece_cols)
    gain_own = norm_gain[0]
    down_other, gain_other = from_partner((down_half, gain_own), "section", 0)
    down_low, down_high = both_halves(down_half, down_other, pair_side)
    gain_low, gain_high = both_halves(gain_own, gain_other, pair_side)
    gain_low = gain_low.astype(jnp.float32)[None, :]
    gain_high = gain_high.astype(jnp.float32)[None, :]
    seg_hit = segment_ids[:, :, None] == lax.broadcasted_iota(
        jnp.int32, (1, 1, segment_job.shape[1]), 2
    )
    token_job = jnp.sum(jnp.where(seg_hit, segment_job[:, None, :], 0), axis=2)
    job_hit = token_job[:, :, None] == lax.broadcasted_iota(
        jnp.int32, (1, 1, job_adapter.shape[0]), 2
    )
    token_adapter = jnp.sum(jnp.where(job_hit, job_adapter[None, None, :], 0), axis=2)
    slot_of_column = lax.broadcasted_iota(jnp.int32, (1, rank_cols), 1) // R
    zero_piece = jnp.zeros((unit_rows, piece_cols), jnp.bfloat16)
    zero_rank = jnp.zeros((unit_rows, rank_cols), jnp.float32)
    results = jnp.zeros((unit_count * unit_rows, piece_cols), jnp.bfloat16)

    def pipe_step(step_turn, carry):
        incoming, incoming_other, results = carry
        unit_index = step_turn - section_level
        active = jnp.logical_and(unit_index >= 0, unit_index < unit_count)
        unit_slot = jnp.clip(unit_index, 0, unit_count - 1)
        source = lax.dynamic_slice_in_dim(
            hidden_in, jnp.clip(step_turn, 0, unit_count - 1) * unit_rows, unit_rows, 0
        )
        own_source = lax.dynamic_slice_in_dim(source, pair_side * piece_cols, piece_cols, 1)
        own_piece = jnp.where(section_level == 0, own_source, incoming)
        other_piece = from_partner(own_piece, "section", 0)
        own_half, other_half = side_by_side((own_piece, other_piece), "tensor", 1, 0)
        half_low, half_high = both_halves(own_half, other_half, pair_side)
        low_values = half_low.astype(jnp.float32)
        high_values = half_high.astype(jnp.float32)
        mean_square = (
            jnp.sum(low_values * low_values, axis=1) + jnp.sum(high_values * high_values, axis=1)
        ) / full_width
        row_scale = lax.rsqrt(mean_square + epsilon)[:, None]
        normed_low = (low_values * row_scale * gain_low).astype(jnp.bfloat16)
        normed_high = (high_values * row_scale * gain_high).astype(jnp.bfloat16)
        unit_adapter = lax.dynamic_index_in_dim(token_adapter, unit_slot, 0, keepdims=False)
        keep_mask = slot_of_column == unit_adapter[:, None]
        projected = lax.cond(
            active,
            lambda: product(normed_low, down_low) + product(normed_high, down_high),
            lambda: zero_rank,
        )
        kept_rank = jnp.where(keep_mask, projected, 0.0).astype(jnp.bfloat16)

        def compute():
            frozen_out = product(normed_low, weight_low) + product(normed_high, weight_high)
            adapted = product(kept_rank, up_own)
            return (own_piece.astype(jnp.float32) + frozen_out + adapted).astype(jnp.bfloat16)

        fresh_piece = lax.cond(active, compute, lambda: zero_piece)
        previous = lax.dynamic_slice_in_dim(results, unit_slot * unit_rows, unit_rows, 0)
        results = lax.dynamic_update_slice_in_dim(
            results, jnp.where(active, fresh_piece, previous), unit_slot * unit_rows, 0
        )
        moved_piece = shifted(fresh_piece, "section", 2)
        return (moved_piece, incoming_other, results)

    carry = lax.fori_loop(0, unit_count + levels - 1, pipe_step, (zero_piece, zero_piece, results))
    return carry[2][None]


def solution(mesh):
    return jax.shard_map(
        local,
        mesh=mesh,
        in_specs=(
            P(None, "tensor"),
            P(),
            P(),
            P(),
            P("section"),
            P("section", None, "tensor"),
            P("section", None),
            P("section", "tensor", None, None),
            P("section", "tensor", None, None),
        ),
        out_specs=P("section", None, "tensor"),
        check_vma=False,
    )
```

profile of v0, /device:TPU:62, one launch (start us, length us, event | category | flops | bytes accessed | tf_op | source)
XLA Modules:
  0.0 724.2 jit_solution(11403315338042876360)
XLA Ops:
  9.7 88.9 %all-reduce.3.cloned.1.call-done = (bf16[4096,128]{1,0:T(8,128)(2,1)}, bf16[128,4096]{1,0:T(8,128)(2,1)}) async-done(((bf16[4096,128]{1,0:T(8,128)(2,1)}, bf16[128,4096]{1,0:T(8,128)(2,1)}), (bf16[4096,128]{1,0:T(8,128)(2,1)}, bf16[128,4096]{1,0:T(8,128)(2,1)})) %all-reduce.3.cloned.1.call-update) | async-done | bytes 2097168 | tf_op jit(solution)/shard_map/psum | solution.py:12
  98.9 5.8 fusion.12
  105.8 17.8 %collective-permute-done.3 = bf16[4096,128]{1,0:T(8,128)(2,1)} collective-permute-done((bf16[4096,128]{1,0:T(8,128)(2,1)}, bf16[4096,128]{1,0:T(8,128)(2,1)}, u32[]{:S(2)}, u32[]{:S(2)}) %collective-permute-start.3) | collective-permute-done | bytes 1048608 | tf_op jit(solution)/shard_map/ppermute | solution.py:18
  125.0 591.6 %while.19 = (s32[]{:T(128)}, bf16[32,512]{1,0:T(8,128)(2,1)S(1)}, bf16[128,512]{1,0:T(8,128)(2,1)S(1)}, s32[]{:T(128)}, pred[]{:T(512)}, /*index=5*/pred[]{:T(51...) while((s32[]{:T(128)}, bf16[32,512]{1,0:T(8,128)(2,1)S(1)}, ...), condition=%wide.region_11.12_spmd.clone, body=%wide.region_4.11_spmd.clone.sunk | while | flops 342361152 | bytes 31623924 | solution.py:132
  126.4 3.6 collective-permute-done
  129.9 15.0 %all_gather.13 = bf16[64,4096]{1,0:T(8,128)(2,1)S(1)} all-gather(bf16[64,512]{1,0:T(8,128)(2,1)S(1)} %pad_maximum_fusion.2), channel_id=1, replica_groups=mesh['section'=32,'tensor'=8] {'tensor'}, dimensions={1}, use_global_device_ids=true | all-gather | bytes 589824 | tf_op jit(solution)/shard_map/while/body/eval_jaxpr/all_gather | solution.py:27
  146.8 4.5 collective-permute-done.1
  153.3 2.9 collective-permute-done
  156.2 15.0 %all_gather.13 = bf16[64,4096]{1,0:T(8,128)(2,1)S(1)} all-gather(bf16[64,512]{1,0:T(8,128)(2,1)S(1)} %pad_maximum_fusion.2), channel_id=1, replica_groups=mesh['section'=32,'tensor'=8] {'tensor'}, dimensions={1}, use_global_device_ids=true | all-gather | bytes 589824 | tf_op jit(solution)/shard_map/while/body/eval_jaxpr/all_gather | solution.py:27
  173.1 4.5 collective-permute-done.1
  182.6 15.2 %all_gather.13 = bf16[64,4096]{1,0:T(8,128)(2,1)S(1)} all-gather(bf16[64,512]{1,0:T(8,128)(2,1)S(1)} %pad_maximum_fusion.2), channel_id=1, replica_groups=mesh['section'=32,'tensor'=8] {'tensor'}, dimensions={1}, use_global_device_ids=true | all-gather | bytes 589824 | tf_op jit(solution)/shard_map/while/body/eval_jaxpr/all_gather | solution.py:27
  199.7 4.5 collective-permute-done.1
  209.3 15.3 %all_gather.13 = bf16[64,4096]{1,0:T(8,128)(2,1)S(1)} all-gather(bf16[64,512]{1,0:T(8,128)(2,1)S(1)} %pad_maximum_fusion.2), channel_id=1, replica_groups=mesh['section'=32,'tensor'=8] {'tensor'}, dimensions={1}, use_global_device_ids=true | all-gather | bytes 589824 | tf_op jit(solution)/shard_map/while/body/eval_jaxpr/all_gather | solution.py:27
  226.5 4.5 collective-permute-done.1
  231.8 2.3 collective-permute-start
  236.0 15.4 %all_gather.13 = bf16[64,4096]{1,0:T(8,128)(2,1)S(1)} all-gather(bf16[64,512]{1,0:T(8,128)(2,1)S(1)} %pad_maximum_fusion.2), channel_id=1, replica_groups=mesh['section'=32,'tensor'=8] {'tensor'}, dimensions={1}, use_global_device_ids=true | all-gather | bytes 589824 | tf_op jit(solution)/shard_map/while/body/eval_jaxpr/all_gather | solution.py:27
  253.3 4.6 collective-permute-done.1
  263.0 15.3 %all_gather.13 = bf16[64,4096]{1,0:T(8,128)(2,1)S(1)} all-gather(bf16[64,512]{1,0:T(8,128)(2,1)S(1)} %pad_maximum_fusion.2), channel_id=1, replica_groups=mesh['section'=32,'tensor'=8] {'tensor'}, dimensions={1}, use_global_device_ids=true | all-gather | bytes 589824 | tf_op jit(solution)/shard_map/while/body/eval_jaxpr/all_gather | solution.py:27
  280.1 6.8 collective-permute-done.1
  292.0 15.2 %all_gather.13 = bf16[64,4096]{1,0:T(8,128)(2,1)S(1)} all-gather(bf16[64,512]{1,0:T(8,128)(2,1)S(1)} %pad_maximum_fusion.2), channel_id=1, replica_groups=mesh['section'=32,'tensor'=8] {'tensor'}, dimensions={1}, use_global_device_ids=true | all-gather | bytes 589824 | tf_op jit(solution)/shard_map/while/body/eval_jaxpr/all_gather | solution.py:27
  309.1 6.6 collective-permute-done.1
  316.5 2.4 collective-permute-start
  320.8 15.2 %all_gather.13 = bf16[64,4096]{1,0:T(8,128)(2,1)S(1)} all-gather(bf16[64,512]{1,0:T(8,128)(2,1)S(1)} %pad_maximum_fusion.2), channel_id=1, replica_groups=mesh['section'=32,'tensor'=8] {'tensor'}, dimensions={1}, use_global_device_ids=true | all-gather | bytes 589824 | tf_op jit(solution)/shard_map/while/body/eval_jaxpr/all_gather | solution.py:27
  337.9 6.6 collective-permute-done.1
  345.4 2.3 collective-permute-start
  349.7 15.3 %all_gather.13 = bf16[64,4096]{1,0:T(8,128)(2,1)S(1)} all-gather(bf16[64,512]{1,0:T(8,128)(2,1)S(1)} %pad_maximum_fusion.2), channel_id=1, replica_groups=mesh['section'=32,'tensor'=8] {'tensor'}, dimensions={1}, use_global_device_ids=true | all-gather | bytes 589824 | tf_op jit(solution)/shard_map/while/body/eval_jaxpr/all_gather | solution.py:27
  366.8 6.6 collective-permute-done.1
  374.3 2.4 collective-permute-start
  378.6 15.2 %all_gather.13 = bf16[64,4096]{1,0:T(8,128)(2,1)S(1)} all-gather(bf16[64,512]{1,0:T(8,128)(2,1)S(1)} %pad_maximum_fusion.2), channel_id=1, replica_groups=mesh['section'=32,'tensor'=8] {'tensor'}, dimensions={1}, use_global_device_ids=true | all-gather | bytes 589824 | tf_op jit(solution)/shard_map/while/body/eval_jaxpr/all_gather | solution.py:27
  395.7 6.7 collective-permute-done.1
  403.3 2.3 collective-permute-start
  407.5 15.2 %all_gather.13 = bf16[64,4096]{1,0:T(8,128)(2,1)S(1)} all-gather(bf16[64,512]{1,0:T(8,128)(2,1)S(1)} %pad_maximum_fusion.2), channel_id=1, replica_groups=mesh['section'=32,'tensor'=8] {'tensor'}, dimensions={1}, use_global_device_ids=true | all-gather | bytes 589824 | tf_op jit(solution)/shard_map/while/body/eval_jaxpr/all_gather | solution.py:27
  424.6 6.8 collective-permute-done.1
  432.3 2.3 collective-permute-start
  436.5 15.3 %all_gather.13 = bf16[64,4096]{1,0:T(8,128)(2,1)S(1)} all-gather(bf16[64,512]{1,0:T(8,128)(2,1)S(1)} %pad_maximum_fusion.2), channel_id=1, replica_groups=mesh['section'=32,'tensor'=8] {'tensor'}, dimensions={1}, use_global_device_ids=true | all-gather | bytes 589824 | tf_op jit(solution)/shard_map/while/body/eval_jaxpr/all_gather | solution.py:27
  453.7 6.4 collective-permute-done.1
  460.9 2.3 collective-permute-start
  465.2 15.5 %all_gather.13 = bf16[64,4096]{1,0:T(8,128)(2,1)S(1)} all-gather(bf16[64,512]{1,0:T(8,128)(2,1)S(1)} %pad_maximum_fusion.2), channel_id=1, replica_groups=mesh['section'=32,'tensor'=8] {'tensor'}, dimensions={1}, use_global_device_ids=true | all-gather | bytes 589824 | tf_op jit(solution)/shard_map/while/body/eval_jaxpr/all_gather | solution.py:27
  482.6 6.1 collective-permute-done.1
  489.6 2.3 collective-permute-start
  493.8 15.4 %all_gather.13 = bf16[64,4096]{1,0:T(8,128)(2,1)S(1)} all-gather(bf16[64,512]{1,0:T(8,128)(2,1)S(1)} %pad_maximum_fusion.2), channel_id=1, replica_groups=mesh['section'=32,'tensor'=8] {'tensor'}, dimensions={1}, use_global_device_ids=true | all-gather | bytes 589824 | tf_op jit(solution)/shard_map/while/body/eval_jaxpr/all_gather | solution.py:27
  511.1 6.1 collective-permute-done.1
  522.3 15.5 %all_gather.13 = bf16[64,4096]{1,0:T(8,128)(2,1)S(1)} all-gather(bf16[64,512]{1,0:T(8,128)(2,1)S(1)} %pad_maximum_fusion.2), channel_id=1, replica_groups=mesh['section'=32,'tensor'=8] {'tensor'}, dimensions={1}, use_global_device_ids=true | all-gather | bytes 589824 | tf_op jit(solution)/shard_map/while/body/eval_jaxpr/all_gather | solution.py:27
  539.6 44.4 %collective-permute-done.1 = bf16[32,512]{1,0:T(8,128)(2,1)S(1)} collective-permute-done((bf16[32,512]{1,0:T(8,128)(2,1)S(1)}, bf16[32,512]{1,0:T(8,128)(2,1)S(1)}, u32[]{:S(2)}, u32[]{:S(2)}) %collective-permute-start.1) | collective-permute-done | bytes 32800 | tf_op jit(solution)/shard_map/while/body/eval_jaxpr/ppermute | solution.py:33
  585.0 3.8 collective-permute-done
  588.9 15.4 %all_gather.13 = bf16[64,4096]{1,0:T(8,128)(2,1)S(1)} all-gather(bf16[64,512]{1,0:T(8,128)(2,1)S(1)} %pad_maximum_fusion.2), channel_id=1, replica_groups=mesh['section'=32,'tensor'=8] {'tensor'}, dimensions={1}, use_global_device_ids=true | all-gather | bytes 589824 | tf_op jit(solution)/shard_map/while/body/eval_jaxpr/all_gather | solution.py:27
  605.4 4.4 conditional.7
  605.4 3.1 fusion.14
  611.2 6.5 collective-permute-done.1
  618.7 3.8 collective-permute-done
  622.6 15.4 %all_gather.13 = bf16[64,4096]{1,0:T(8,128)(2,1)S(1)} all-gather(bf16[64,512]{1,0:T(8,128)(2,1)S(1)} %pad_maximum_fusion.2), channel_id=1, replica_groups=mesh['section'=32,'tensor'=8] {'tensor'}, dimensions={1}, use_global_device_ids=true | all-gather | bytes 589824 | tf_op jit(solution)/shard_map/while/body/eval_jaxpr/all_gather | solution.py:27
  639.1 4.4 conditional.7
  639.1 3.1 fusion.14
  644.8 6.5 collective-permute-done.1
  652.4 3.8 collective-permute-done
  656.2 15.4 %all_gather.13 = bf16[64,4096]{1,0:T(8,128)(2,1)S(1)} all-gather(bf16[64,512]{1,0:T(8,128)(2,1)S(1)} %pad_maximum_fusion.2), channel_id=1, replica_groups=mesh['section'=32,'tensor'=8] {'tensor'}, dimensions={1}, use_global_device_ids=true | all-gather | bytes 589824 | tf_op jit(solution)/shard_map/while/body/eval_jaxpr/all_gather | solution.py:27
  672.8 4.4 conditional.7
  672.8 3.1 fusion.14
  678.5 6.5 collective-permute-done.1
  686.1 3.8 collective-permute-done
  689.9 15.4 %all_gather.13 = bf16[64,4096]{1,0:T(8,128)(2,1)S(1)} all-gather(bf16[64,512]{1,0:T(8,128)(2,1)S(1)} %pad_maximum_fusion.2), channel_id=1, replica_groups=mesh['section'=32,'tensor'=8] {'tensor'}, dimensions={1}, use_global_device_ids=true | all-gather | bytes 589824 | tf_op jit(solution)/shard_map/while/body/eval_jaxpr/all_gather | solution.py:27
  706.4 4.4 conditional.7
  706.4 3.1 fusion.14
  712.2 4.5 collective-permute-done.1
  (329 shorter events, 105.0 us)
Async XLA Ops:
  6.5 2.9 copy-start.3
  6.5 92.2 %copy-start.5 = (s32[4,32]{1,0:T(4,128)S(1)}, s32[4,32]{1,0:T(4,128)}, u32[]{:S(2)}) copy-start(s32[4,32]{1,0:T(4,128)} %param.16) | copy-start | bytes 1540
  6.5 92.2 %copy-start.4 = (s32[4,8]{1,0:T(4,128)S(1)}, s32[4,8]{1,0:T(4,128)}, u32[]{:S(2)}) copy-start(s32[4,8]{1,0:T(4,128)} %param.17) | copy-start | bytes 388
  6.5 92.0 %all-reduce.3.cloned.1.call-start = ((), (), s32[]{:S(2)}) async-start(), calls=%async_computation | async-start | bytes 4194304 | tf_op jit(solution)/shard_map/psum | solution.py:12
  9.5 95.4 %collective-permute-start.2 = (bf16[4096]{0:T(1024)(128)(2,1)S(1)}, bf16[4096]{0:T(1024)(128)(2,1)S(1)}, u32[]{:S(2)}, u32[]{:S(2)}) collective-permute-start(bf16[4096]{0:T(1024)(128)(2,1)S(1)} %reduce), channel_id=1, source_target_pairs={{0,8},{8,0},{16,24},{24,16},{32,40},{40,32},{48,56},{56,48},{64,72... | collective-permute-start | bytes 24584 | tf_op jit(solution)/shard_map/ppermute | solution.py:18
  98.5 25.1 %collective-permute-start.3 = (bf16[4096,128]{1,0:T(8,128)(2,1)}, bf16[4096,128]{1,0:T(8,128)(2,1)}, u32[]{:S(2)}, u32[]{:S(2)}) collective-permute-start(bf16[4096,128]{1,0:T(8,128)(2,1)} %get-tuple-element.551), channel_id=1, source_target_pairs={{0,8},{8,0},{16,24},{24,16},{32,40},{40,32},{48,56},{56,48},{64,72... | collective-permute-start | bytes 3145736 | tf_op jit(solution)/shard_map/ppermute | solution.py:18
  98.9 5.9 copy-start.6
  98.9 24.7 %copy-start.1 = (bf16[4096,128]{1,0:T(8,128)(2,1)S(1)}, bf16[4096,128]{1,0:T(8,128)(2,1)}, u32[]{:S(2)}) copy-start(bf16[4096,128]{1,0:T(8,128)(2,1)} %get-tuple-element.551) | copy-start | bytes 3145732
  125.9 4.0 collective-permute-start
  145.5 5.8 collective-permute-start.1
  152.2 4.0 collective-permute-start
  171.8 5.8 collective-permute-start.1
  178.5 4.1 collective-permute-start
  198.4 5.8 collective-permute-start.1
  205.1 4.2 collective-permute-start
  225.1 5.8 collective-permute-start.1
  231.8 4.2 collective-permute-start
  252.0 6.0 collective-permute-start.1
  258.8 4.2 collective-permute-start
  278.8 8.1 %collective-permute-start.1 = (bf16[32,512]{1,0:T(8,128)(2,1)S(1)}, bf16[32,512]{1,0:T(8,128)(2,1)S(1)}, u32[]{:S(2)}, u32[]{:S(2)}) collective-permute-start(bf16[32,512]{1,0:T(8,128)(2,1)S(1)} %get-tuple-element.738), channel_id=1, source_target_pairs={{0,16},{8,24},{16,32},{24,40},{32,48},{40,56},{48,64},{56,72},{64,... | collective-permute-start | bytes 98312 | tf_op jit(solution)/shard_map/while/body/eval_jaxpr/ppermute | solution.py:33
  287.8 4.2 collective-permute-start
  307.8 7.9 %collective-permute-start.1 = (bf16[32,512]{1,0:T(8,128)(2,1)S(1)}, bf16[32,512]{1,0:T(8,128)(2,1)S(1)}, u32[]{:S(2)}, u32[]{:S(2)}) collective-permute-start(bf16[32,512]{1,0:T(8,128)(2,1)S(1)} %get-tuple-element.738), channel_id=1, source_target_pairs={{0,16},{8,24},{16,32},{24,40},{32,48},{40,56},{48,64},{56,72},{64,... | collective-permute-start | bytes 98312 | tf_op jit(solution)/shard_map/while/body/eval_jaxpr/ppermute | solution.py:33
  316.5 4.3 collective-permute-start
  336.6 7.9 %collective-permute-start.1 = (bf16[32,512]{1,0:T(8,128)(2,1)S(1)}, bf16[32,512]{1,0:T(8,128)(2,1)S(1)}, u32[]{:S(2)}, u32[]{:S(2)}) collective-permute-start(bf16[32,512]{1,0:T(8,128)(2,1)S(1)} %get-tuple-element.738), channel_id=1, source_target_pairs={{0,16},{8,24},{16,32},{24,40},{32,48},{40,56},{48,64},{56,72},{64,... | collective-permute-start | bytes 98312 | tf_op jit(solution)/shard_map/while/body/eval_jaxpr/ppermute | solution.py:33
  345.4 4.2 collective-permute-start
  365.5 7.9 %collective-permute-start.1 = (bf16[32,512]{1,0:T(8,128)(2,1)S(1)}, bf16[32,512]{1,0:T(8,128)(2,1)S(1)}, u32[]{:S(2)}, u32[]{:S(2)}) collective-permute-start(bf16[32,512]{1,0:T(8,128)(2,1)S(1)} %get-tuple-element.738), channel_id=1, source_target_pairs={{0,16},{8,24},{16,32},{24,40},{32,48},{40,56},{48,64},{56,72},{64,... | collective-permute-start | bytes 98312 | tf_op jit(solution)/shard_map/while/body/eval_jaxpr/ppermute | solution.py:33
  374.3 4.2 collective-permute-start
  394.4 8.0 %collective-permute-start.1 = (bf16[32,512]{1,0:T(8,128)(2,1)S(1)}, bf16[32,512]{1,0:T(8,128)(2,1)S(1)}, u32[]{:S(2)}, u32[]{:S(2)}) collective-permute-start(bf16[32,512]{1,0:T(8,128)(2,1)S(1)} %get-tuple-element.738), channel_id=1, source_target_pairs={{0,16},{8,24},{16,32},{24,40},{32,48},{40,56},{48,64},{56,72},{64,... | collective-permute-start | bytes 98312 | tf_op jit(solution)/shard_map/while/body/eval_jaxpr/ppermute | solution.py:33
  403.3 4.2 collective-permute-start
  423.3 8.1 %collective-permute-start.1 = (bf16[32,512]{1,0:T(8,128)(2,1)S(1)}, bf16[32,512]{1,0:T(8,128)(2,1)S(1)}, u32[]{:S(2)}, u32[]{:S(2)}) collective-permute-start(bf16[32,512]{1,0:T(8,128)(2,1)S(1)} %get-tuple-element.738), channel_id=1, source_target_pairs={{0,16},{8,24},{16,32},{24,40},{32,48},{40,56},{48,64},{56,72},{64,... | collective-permute-start | bytes 98312 | tf_op jit(solution)/shard_map/while/body/eval_jaxpr/ppermute | solution.py:33
  432.3 4.2 collective-permute-start
  452.4 7.7 %collective-permute-start.1 = (bf16[32,512]{1,0:T(8,128)(2,1)S(1)}, bf16[32,512]{1,0:T(8,128)(2,1)S(1)}, u32[]{:S(2)}, u32[]{:S(2)}) collective-permute-start(bf16[32,512]{1,0:T(8,128)(2,1)S(1)} %get-tuple-element.738), channel_id=1, source_target_pairs={{0,16},{8,24},{16,32},{24,40},{32,48},{40,56},{48,64},{56,72},{64,... | collective-permute-start | bytes 98312 | tf_op jit(solution)/shard_map/while/body/eval_jaxpr/ppermute | solution.py:33
  460.9 4.2 collective-permute-start
  481.3 7.4 %collective-permute-start.1 = (bf16[32,512]{1,0:T(8,128)(2,1)S(1)}, bf16[32,512]{1,0:T(8,128)(2,1)S(1)}, u32[]{:S(2)}, u32[]{:S(2)}) collective-permute-start(bf16[32,512]{1,0:T(8,128)(2,1)S(1)} %get-tuple-element.738), channel_id=1, source_target_pairs={{0,16},{8,24},{16,32},{24,40},{32,48},{40,56},{48,64},{56,72},{64,... | collective-permute-start | bytes 98312 | tf_op jit(solution)/shard_map/while/body/eval_jaxpr/ppermute | solution.py:33
  489.6 4.2 collective-permute-start
  509.8 7.4 %collective-permute-start.1 = (bf16[32,512]{1,0:T(8,128)(2,1)S(1)}, bf16[32,512]{1,0:T(8,128)(2,1)S(1)}, u32[]{:S(2)}, u32[]{:S(2)}) collective-permute-start(bf16[32,512]{1,0:T(8,128)(2,1)S(1)} %get-tuple-element.738), channel_id=1, source_target_pairs={{0,16},{8,24},{16,32},{24,40},{32,48},{40,56},{48,64},{56,72},{64,... | collective-permute-start | bytes 98312 | tf_op jit(solution)/shard_map/while/body/eval_jaxpr/ppermute | solution.py:33
  518.1 4.2 collective-permute-start
  538.3 45.7 %collective-permute-start.1 = (bf16[32,512]{1,0:T(8,128)(2,1)S(1)}, bf16[32,512]{1,0:T(8,128)(2,1)S(1)}, u32[]{:S(2)}, u32[]{:S(2)}) collective-permute-start(bf16[32,512]{1,0:T(8,128)(2,1)S(1)} %get-tuple-element.738), channel_id=1, source_target_pairs={{0,16},{8,24},{16,32},{24,40},{32,48},{40,56},{48,64},{56,72},{64,... | collective-permute-start | bytes 98312 | tf_op jit(solution)/shard_map/while/body/eval_jaxpr/ppermute | solution.py:33
  584.9 4.0 collective-permute-start
  605.4 3.5 copy-start
  609.8 7.9 %collective-permute-start.1 = (bf16[32,512]{1,0:T(8,128)(2,1)S(1)}, bf16[32,512]{1,0:T(8,128)(2,1)S(1)}, u32[]{:S(2)}, u32[]{:S(2)}) collective-permute-start(bf16[32,512]{1,0:T(8,128)(2,1)S(1)} %get-tuple-element.738), channel_id=1, source_target_pairs={{0,16},{8,24},{16,32},{24,40},{32,48},{40,56},{48,64},{56,72},{64,... | collective-permute-start | bytes 98312 | tf_op jit(solution)/shard_map/while/body/eval_jaxpr/ppermute | solution.py:33
  618.6 4.0 collective-permute-start
  639.1 3.5 copy-start
  643.5 7.9 %collective-permute-start.1 = (bf16[32,512]{1,0:T(8,128)(2,1)S(1)}, bf16[32,512]{1,0:T(8,128)(2,1)S(1)}, u32[]{:S(2)}, u32[]{:S(2)}) collective-permute-start(bf16[32,512]{1,0:T(8,128)(2,1)S(1)} %get-tuple-element.738), channel_id=1, source_target_pairs={{0,16},{8,24},{16,32},{24,40},{32,48},{40,56},{48,64},{56,72},{64,... | collective-permute-start | bytes 98312 | tf_op jit(solution)/shard_map/while/body/eval_jaxpr/ppermute | solution.py:33
  652.2 4.0 collective-permute-start
  672.8 3.5 copy-start
  677.2 7.9 %collective-permute-start.1 = (bf16[32,512]{1,0:T(8,128)(2,1)S(1)}, bf16[32,512]{1,0:T(8,128)(2,1)S(1)}, u32[]{:S(2)}, u32[]{:S(2)}) collective-permute-start(bf16[32,512]{1,0:T(8,128)(2,1)S(1)} %get-tuple-element.738), channel_id=1, source_target_pairs={{0,16},{8,24},{16,32},{24,40},{32,48},{40,56},{48,64},{56,72},{64,... | collective-permute-start | bytes 98312 | tf_op jit(solution)/shard_map/while/body/eval_jaxpr/ppermute | solution.py:33
  685.9 4.0 collective-permute-start
  706.4 3.5 copy-start
  710.9 5.8 collective-permute-start.1
  716.7 0.7 copy-start.2
Sparse Core Ops, SparseCore 0:
  10.0 88.4 all-reduce.2
where the time goes:
time: 726 us; the launch traced here: 724 us
  waiting for transfers between devices  303 us (42%)
  blocking collectives  291 us (40%)
  starting transfers between devices  56.9 us (8%)
  other arithmetic  30.6 us (4%)
  matrix products  18.6 us (3%)
  between operations  14.2 us (2%)
  local copies, waits for them, and re-layouts  8.94 us (1%)
    all_gather x19, blocking collectives, side_by_side(): lax.all_gather(both, axis, axis=dim, tiled=True)  291 us
    ppermute x19, waiting for transfers between devices, shifted(): lax.ppermute(value, axis, [(source, source + steps) for source in range(f...  150 us
    psum x1, waiting for transfers between devices, spread(): return lax.psum(block, axis)  88.9 us
    ppermute x21, waiting for transfers between devices, from_partner(): return lax.ppermute(value, axis, pairs)  63.9 us
    ppermute x21, starting transfers between devices, from_partner(): return lax.ppermute(value, axis, pairs)  32.3 us
    ppermute x19, starting transfers between devices, shifted(): lax.ppermute(value, axis, [(source, source + steps) for source in range(f...  24.6 us
    dot_general x20, matrix products, product(): return jnp.dot(left, right, preferred_element_type=jnp.float32)  18.6 us
    select_n x19, other arithmetic, pipe_step(): own_piece = jnp.where(section_level == 0, own_source, incoming)  16.1 us
  transfers between devices with their start and end apart: 41, of which 40 were waited for; matrix products, arithmetic and copies ran while one was open for 1% of the time, Pallas kernels for 0%

commit v1 on v0

--- a/solution.py
+++ b/solution.py
@@ -9,7 +9,7 @@
 
 def spread(block, axis, owner):
     block = jnp.where(lax.axis_index(axis) == owner, block, jnp.zeros_like(block))
-    return lax.psum(block, axis)
+    return jnp.sum(lax.all_gather(block, axis), axis=0)
 
 
 def from_partner(value, axis, bit):

time: 726 us -> 812 us (1.12)
  waiting for transfers between devices: 303 us -> 374 us
  other arithmetic: 30.6 us -> 41.1 us
    all_gather x0 -> x2, waiting for transfers between devices: none -> 179 us  [spread(): return jnp.sum(lax.all_gather(block, axis), axis=0)]
    psum x1 -> x0, waiting for transfers between devices: 88.9 us -> none  [spread(): return lax.psum(block, axis)]
    ppermute x21, waiting for transfers between devices: 63.9 us -> 42.4 us  [from_partner(): return lax.ppermute(value, axis, pairs)]
    reduce_sum x0 -> x2, other arithmetic: none -> 10.1 us  [spread(): return jnp.sum(lax.all_gather(block, axis), axis=0)]
  transfers between devices with their start and end apart: 41 -> 42, of which waited for: 40 -> 40; matrix products, arithmetic and copies ran while one was open for 1% -> 2% of each run, Pallas kernels for 0% -> 0%
where the time goes in v1:
time: 812 us; the launch traced here: 808 us
  waiting for transfers between devices  374 us (46%)
  blocking collectives  290 us (36%)
  starting transfers between devices  61 us (8%)
  other arithmetic  41.1 us (5%)
  matrix products  18.6 us (2%)
  between operations  14.2 us (2%)
    all_gather x19, blocking collectives, side_by_side(): lax.all_gather(both, axis, axis=dim, tiled=True)  290 us
    all_gather x2, waiting for transfers between devices, spread(): return jnp.sum(lax.all_gather(block, axis), axis=0)  179 us
    ppermute x19, waiting for transfers between devices, shifted(): lax.ppermute(value, axis, [(source, source + steps) for source in range(f...  152 us
    ppermute x21, waiting for transfers between devices, from_partner(): return lax.ppermute(value, axis, pairs)  42.4 us
    ppermute x21, starting transfers between devices, from_partner(): return lax.ppermute(value, axis, pairs)  36.4 us
    ppermute x19, starting transfers between devices, shifted(): lax.ppermute(value, axis, [(source, source + steps) for source in range(f...  24.6 us
    dot_general x20, matrix products, product(): return jnp.dot(left, right, preferred_element_type=jnp.float32)  18.6 us
  transfers between devices with their start and end apart: 42, of which 40 were waited for; matrix products, arithmetic and copies ran while one was open for 2% of the time, Pallas kernels for 0%

profile of v1, /device:TPU:62, one launch (start us, length us, event | category | flops | bytes accessed | tf_op | source)
XLA Modules:
  0.0 807.9 jit_solution(6684304179830756334)
XLA Ops:
  9.8 89.4 %all-gather.5.cloned.1.call-done = bf16[8,1,4096,128]{3,2,1,0:T(8,128)(2,1)} async-done(((bf16[1,1,4096,128]{3,2,1,0:T(8,128)(2,1)}), bf16[8,1,4096,128]{3,2,1,0:T(8,128)(2,1)}) %all-gather.5.cloned.1.call-update) | async-done | bytes 8388624 | tf_op jit(solution)/shard_map/all_gather | solution.py:12
  99.2 5.2 reduce_sum.78
  104.6 5.9 fusion.12
  110.6 89.5 %all-gather.7.cloned.1.call-done = bf16[8,1,128,4096]{3,2,1,0:T(8,128)(2,1)} async-done(((bf16[1,1,128,4096]{3,2,1,0:T(8,128)(2,1)}), bf16[8,1,128,4096]{3,2,1,0:T(8,128)(2,1)}) %all-gather.7.cloned.1.call-update) | async-done | bytes 8388624 | tf_op jit(solution)/shard_map/all_gather | solution.py:12
  200.1 4.9 reduce_sum.79
  206.8 593.7 %while.19 = (s32[]{:T(128)}, bf16[32,512]{1,0:T(8,128)(2,1)S(1)}, bf16[128,512]{1,0:T(8,128)(2,1)S(1)}, s32[]{:T(128)}, pred[]{:T(512)}, /*index=5*/pred[]{:T(51...) while((s32[]{:T(128)}, bf16[32,512]{1,0:T(8,128)(2,1)S(1)}, ...), condition=%wide.region_11.12_spmd.clone, body=%wide.region_4.11_spmd.clone.sunk | while | flops 342361152 | bytes 31623924 | solution.py:132
  207.8 3.8 collective-permute-done
  211.7 15.2 %all_gather.23 = bf16[64,4096]{1,0:T(8,128)(2,1)S(1)} all-gather(bf16[64,512]{1,0:T(8,128)(2,1)S(1)} %pad_maximum_fusion.2), channel_id=1, replica_groups=mesh['section'=32,'tensor'=8] {'tensor'}, dimensions={1}, use_global_device_ids=true | all-gather | bytes 589824 | tf_op jit(solution)/shard_map/while/body/eval_jaxpr/all_gather | solution.py:27
  228.8 4.5 collective-permute-done.1
  235.5 2.6 collective-permute-done
  238.2 15.1 %all_gather.23 = bf16[64,4096]{1,0:T(8,128)(2,1)S(1)} all-gather(bf16[64,512]{1,0:T(8,128)(2,1)S(1)} %pad_maximum_fusion.2), channel_id=1, replica_groups=mesh['section'=32,'tensor'=8] {'tensor'}, dimensions={1}, use_global_device_ids=true | all-gather | bytes 589824 | tf_op jit(solution)/shard_map/while/body/eval_jaxpr/all_gather | solution.py:27
  255.2 4.5 collective-permute-done.1
  264.5 15.0 %all_gather.23 = bf16[64,4096]{1,0:T(8,128)(2,1)S(1)} all-gather(bf16[64,512]{1,0:T(8,128)(2,1)S(1)} %pad_maximum_fusion.2), channel_id=1, replica_groups=mesh['section'=32,'tensor'=8] {'tensor'}, dimensions={1}, use_global_device_ids=true | all-gather | bytes 589824 | tf_op jit(solution)/shard_map/while/body/eval_jaxpr/all_gather | solution.py:27
  281.5 4.5 collective-permute-done.1
  286.8 2.7 collective-permute-start
  291.4 14.9 %all_gather.23 = bf16[64,4096]{1,0:T(8,128)(2,1)S(1)} all-gather(bf16[64,512]{1,0:T(8,128)(2,1)S(1)} %pad_maximum_fusion.2), channel_id=1, replica_groups=mesh['section'=32,'tensor'=8] {'tensor'}, dimensions={1}, use_global_device_ids=true | all-gather | bytes 589824 | tf_op jit(solution)/shard_map/while/body/eval_jaxpr/all_gather | solution.py:27
  308.2 4.5 collective-permute-done.1
  313.5 2.8 collective-permute-start
  318.2 14.9 %all_gather.23 = bf16[64,4096]{1,0:T(8,128)(2,1)S(1)} all-gather(bf16[64,512]{1,0:T(8,128)(2,1)S(1)} %pad_maximum_fusion.2), channel_id=1, replica_groups=mesh['section'=32,'tensor'=8] {'tensor'}, dimensions={1}, use_global_device_ids=true | all-gather | bytes 589824 | tf_op jit(solution)/shard_map/while/body/eval_jaxpr/all_gather | solution.py:27
  335.1 5.0 collective-permute-done.1
  345.0 15.2 %all_gather.23 = bf16[64,4096]{1,0:T(8,128)(2,1)S(1)} all-gather(bf16[64,512]{1,0:T(8,128)(2,1)S(1)} %pad_maximum_fusion.2), channel_id=1, replica_groups=mesh['section'=32,'tensor'=8] {'tensor'}, dimensions={1}, use_global_device_ids=true | all-gather | bytes 589824 | tf_op jit(solution)/shard_map/while/body/eval_jaxpr/all_gather | solution.py:27
  362.1 6.5 collective-permute-done.1
  373.5 15.6 %all_gather.23 = bf16[64,4096]{1,0:T(8,128)(2,1)S(1)} all-gather(bf16[64,512]{1,0:T(8,128)(2,1)S(1)} %pad_maximum_fusion.2), channel_id=1, replica_groups=mesh['section'=32,'tensor'=8] {'tensor'}, dimensions={1}, use_global_device_ids=true | all-gather | bytes 589824 | tf_op jit(solution)/shard_map/while/body/eval_jaxpr/all_gather | solution.py:27
  391.0 6.4 collective-permute-done.1
  402.3 15.5 %all_gather.23 = bf16[64,4096]{1,0:T(8,128)(2,1)S(1)} all-gather(bf16[64,512]{1,0:T(8,128)(2,1)S(1)} %pad_maximum_fusion.2), channel_id=1, replica_groups=mesh['section'=32,'tensor'=8] {'tensor'}, dimensions={1}, use_global_device_ids=true | all-gather | bytes 589824 | tf_op jit(solution)/shard_map/while/body/eval_jaxpr/all_gather | solution.py:27
  419.7 6.8 collective-permute-done.1
  428.8 2.5 collective-permute-done
  431.3 15.3 %all_gather.23 = bf16[64,4096]{1,0:T(8,128)(2,1)S(1)} all-gather(bf16[64,512]{1,0:T(8,128)(2,1)S(1)} %pad_maximum_fusion.2), channel_id=1, replica_groups=mesh['section'=32,'tensor'=8] {'tensor'}, dimensions={1}, use_global_device_ids=true | all-gather | bytes 589824 | tf_op jit(solution)/shard_map/while/body/eval_jaxpr/all_gather | solution.py:27
  448.5 6.6 collective-permute-done.1
  460.0 15.5 %all_gather.23 = bf16[64,4096]{1,0:T(8,128)(2,1)S(1)} all-gather(bf16[64,512]{1,0:T(8,128)(2,1)S(1)} %pad_maximum_fusion.2), channel_id=1, replica_groups=mesh['section'=32,'tensor'=8] {'tensor'}, dimensions={1}, use_global_device_ids=true | all-gather | bytes 589824 | tf_op jit(solution)/shard_map/while/body/eval_jaxpr/all_gather | solution.py:27
  477.4 6.5 collective-permute-done.1
  488.8 15.5 %all_gather.23 = bf16[64,4096]{1,0:T(8,128)(2,1)S(1)} all-gather(bf16[64,512]{1,0:T(8,128)(2,1)S(1)} %pad_maximum_fusion.2), channel_id=1, replica_groups=mesh['section'=32,'tensor'=8] {'tensor'}, dimensions={1}, use_global_device_ids=true | all-gather | bytes 589824 | tf_op jit(solution)/shard_map/while/body/eval_jaxpr/all_gather | solution.py:27
  506.2 6.7 collective-permute-done.1
  515.4 2.4 collective-permute-done
  517.8 15.5 %all_gather.23 = bf16[64,4096]{1,0:T(8,128)(2,1)S(1)} all-gather(bf16[64,512]{1,0:T(8,128)(2,1)S(1)} %pad_maximum_fusion.2), channel_id=1, replica_groups=mesh['section'=32,'tensor'=8] {'tensor'}, dimensions={1}, use_global_device_ids=true | all-gather | bytes 589824 | tf_op jit(solution)/shard_map/while/body/eval_jaxpr/all_gather | solution.py:27
  535.2 6.4 collective-permute-done.1
  546.4 15.5 %all_gather.23 = bf16[64,4096]{1,0:T(8,128)(2,1)S(1)} all-gather(bf16[64,512]{1,0:T(8,128)(2,1)S(1)} %pad_maximum_fusion.2), channel_id=1, replica_groups=mesh['section'=32,'tensor'=8] {'tensor'}, dimensions={1}, use_global_device_ids=true | all-gather | bytes 589824 | tf_op jit(solution)/shard_map/while/body/eval_jaxpr/all_gather | solution.py:27
  563.8 6.8 collective-permute-done.1
  573.0 2.4 collective-permute-done
  575.4 15.3 %all_gather.23 = bf16[64,4096]{1,0:T(8,128)(2,1)S(1)} all-gather(bf16[64,512]{1,0:T(8,128)(2,1)S(1)} %pad_maximum_fusion.2), channel_id=1, replica_groups=mesh['section'=32,'tensor'=8] {'tensor'}, dimensions={1}, use_global_device_ids=true | all-gather | bytes 589824 | tf_op jit(solution)/shard_map/while/body/eval_jaxpr/all_gather | solution.py:27
  592.7 6.6 collective-permute-done.1
  601.7 2.4 collective-permute-done
  604.1 15.6 %all_gather.23 = bf16[64,4096]{1,0:T(8,128)(2,1)S(1)} all-gather(bf16[64,512]{1,0:T(8,128)(2,1)S(1)} %pad_maximum_fusion.2), channel_id=1, replica_groups=mesh['section'=32,'tensor'=8] {'tensor'}, dimensions={1}, use_global_device_ids=true | all-gather | bytes 589824 | tf_op jit(solution)/shard_map/while/body/eval_jaxpr/all_gather | solution.py:27
  621.7 45.3 %collective-permute-done.1 = bf16[32,512]{1,0:T(8,128)(2,1)S(1)} collective-permute-done((bf16[32,512]{1,0:T(8,128)(2,1)S(1)}, bf16[32,512]{1,0:T(8,128)(2,1)S(1)}, u32[]{:S(2)}, u32[]{:S(2)}) %collective-permute-start.1) | collective-permute-done | bytes 32800 | tf_op jit(solution)/shard_map/while/body/eval_jaxpr/ppermute | solution.py:33
  667.8 2.6 collective-permute-start
  672.3 14.9 %all_gather.23 = bf16[64,4096]{1,0:T(8,128)(2,1)S(1)} all-gather(bf16[64,512]{1,0:T(8,128)(2,1)S(1)} %pad_maximum_fusion.2), channel_id=1, replica_groups=mesh['section'=32,'tensor'=8] {'tensor'}, dimensions={1}, use_global_device_ids=true | all-gather | bytes 589824 | tf_op jit(solution)/shard_map/while/body/eval_jaxpr/all_gather | solution.py:27
  688.3 4.4 conditional.7
  688.3 3.1 fusion.14
  694.1 7.1 collective-permute-done.1
  702.0 2.5 collective-permute-start
  706.4 14.9 %all_gather.23 = bf16[64,4096]{1,0:T(8,128)(2,1)S(1)} all-gather(bf16[64,512]{1,0:T(8,128)(2,1)S(1)} %pad_maximum_fusion.2), channel_id=1, replica_groups=mesh['section'=32,'tensor'=8] {'tensor'}, dimensions={1}, use_global_device_ids=true | all-gather | bytes 589824 | tf_op jit(solution)/shard_map/while/body/eval_jaxpr/all_gather | solution.py:27
  722.5 4.4 conditional.7
  722.5 3.1 fusion.14
  728.3 6.7 collective-permute-done.1
  735.8 2.6 collective-permute-start
  740.2 15.0 %all_gather.23 = bf16[64,4096]{1,0:T(8,128)(2,1)S(1)} all-gather(bf16[64,512]{1,0:T(8,128)(2,1)S(1)} %pad_maximum_fusion.2), channel_id=1, replica_groups=mesh['section'=32,'tensor'=8] {'tensor'}, dimensions={1}, use_global_device_ids=true | all-gather | bytes 589824 | tf_op jit(solution)/shard_map/while/body/eval_jaxpr/all_gather | solution.py:27
  756.4 4.4 conditional.7
  756.4 3.1 fusion.14
  762.1 6.6 collective-permute-done.1
  769.6 2.6 collective-permute-start
  774.0 15.0 %all_gather.23 = bf16[64,4096]{1,0:T(8,128)(2,1)S(1)} all-gather(bf16[64,512]{1,0:T(8,128)(2,1)S(1)} %pad_maximum_fusion.2), channel_id=1, replica_groups=mesh['section'=32,'tensor'=8] {'tensor'}, dimensions={1}, use_global_device_ids=true | all-gather | bytes 589824 | tf_op jit(solution)/shard_map/while/body/eval_jaxpr/all_gather | solution.py:27
  790.2 4.4 conditional.7
  790.2 3.1 fusion.14
  795.9 4.5 collective-permute-done.1
  (334 shorter events, 113.6 us)
Async XLA Ops:
  6.5 3.0 copy-start.3
  6.5 92.6 %all-gather.5.cloned.1.call-start = ((), (), s32[]{:S(2)}) async-start(), calls=%async_computation | async-start | bytes 9437184 | tf_op jit(solution)/shard_map/all_gather | solution.py:12
  8.3 191.7 %all-gather.7.cloned.1.call-start = ((), (), s32[]{:S(2)}) async-start(), calls=%async_computation.1 | async-start | bytes 9437184 | tf_op jit(solution)/shard_map/all_gather | solution.py:12
  9.5 94.9 %copy-start.4 = (s32[4,8]{1,0:T(4,128)S(1)}, s32[4,8]{1,0:T(4,128)}, u32[]{:S(2)}) copy-start(s32[4,8]{1,0:T(4,128)} %param.17) | copy-start | bytes 388
  9.6 94.9 %copy-start.5 = (s32[4,32]{1,0:T(4,128)S(1)}, s32[4,32]{1,0:T(4,128)}, u32[]{:S(2)}) copy-start(s32[4,32]{1,0:T(4,128)} %param.16) | copy-start | bytes 1540
  9.6 101.0 %collective-permute-start.2 = (bf16[4096]{0:T(1024)(128)(2,1)S(1)}, bf16[4096]{0:T(1024)(128)(2,1)S(1)}, u32[]{:S(2)}, u32[]{:S(2)}) collective-permute-start(bf16[4096]{0:T(1024)(128)(2,1)S(1)} %reduce.4), channel_id=1, source_target_pairs={{0,8},{8,0},{16,24},{24,16},{32,40},{40,32},{48,56},{56,48},{64,72... | collective-permute-start | bytes 24584 | tf_op jit(solution)/shard_map/ppermute | solution.py:18
  104.4 6.1 copy-start.1
  104.4 100.6 %collective-permute-start.3 = (bf16[4096,128]{1,0:T(8,128)(2,1)S(1)}, bf16[4096,128]{1,0:T(8,128)(2,1)}, u32[]{:S(2)}, u32[]{:S(2)}) collective-permute-start(bf16[4096,128]{1,0:T(8,128)(2,1)S(1)} %reduce_sum.78), channel_id=1, source_target_pairs={{0,8},{8,0},{16,24},{24,16},{32,40},{40,32},{48,56},{56,48},{64,72... | collective-permute-start | bytes 3145736 | tf_op jit(solution)/shard_map/ppermute | solution.py:18
  104.6 5.9 copy-start.6
  207.7 4.0 collective-permute-start
  227.5 5.8 collective-permute-start.1
  234.2 4.0 collective-permute-start
  253.8 5.8 collective-permute-start.1
  260.5 4.0 collective-permute-start
  280.1 5.8 collective-permute-start.1
  286.8 4.6 collective-permute-start
  306.8 5.8 collective-permute-start.1
  313.5 4.7 collective-permute-start
  333.8 6.3 collective-permute-start.1
  340.9 4.0 collective-permute-start
  360.8 7.9 collective-permute-start.1
  369.5 4.0 collective-permute-start
  389.7 7.7 collective-permute-start.1
  398.3 4.0 collective-permute-start
  418.3 8.1 %collective-permute-start.1 = (bf16[32,512]{1,0:T(8,128)(2,1)S(1)}, bf16[32,512]{1,0:T(8,128)(2,1)S(1)}, u32[]{:S(2)}, u32[]{:S(2)}) collective-permute-start(bf16[32,512]{1,0:T(8,128)(2,1)S(1)} %get-tuple-element.734), channel_id=1, source_target_pairs={{0,16},{8,24},{16,32},{24,40},{32,48},{40,56},{48,64},{56,72},{64,... | collective-permute-start | bytes 98312 | tf_op jit(solution)/shard_map/while/body/eval_jaxpr/ppermute | solution.py:33
  427.3 4.0 collective-permute-start
  447.2 7.9 collective-permute-start.1
  456.0 4.0 collective-permute-start
  476.1 7.8 collective-permute-start.1
  484.7 4.0 collective-permute-start
  504.8 8.1 collective-permute-start.1
  513.8 4.0 collective-permute-start
  533.9 7.7 collective-permute-start.1
  542.4 4.0 collective-permute-start
  562.5 8.1 %collective-permute-start.1 = (bf16[32,512]{1,0:T(8,128)(2,1)S(1)}, bf16[32,512]{1,0:T(8,128)(2,1)S(1)}, u32[]{:S(2)}, u32[]{:S(2)}) collective-permute-start(bf16[32,512]{1,0:T(8,128)(2,1)S(1)} %get-tuple-element.734), channel_id=1, source_target_pairs={{0,16},{8,24},{16,32},{24,40},{32,48},{40,56},{48,64},{56,72},{64,... | collective-permute-start | bytes 98312 | tf_op jit(solution)/shard_map/while/body/eval_jaxpr/ppermute | solution.py:33
  571.4 4.0 collective-permute-start
  591.3 7.9 collective-permute-start.1
  600.1 4.0 collective-permute-start
  620.3 46.6 %collective-permute-start.1 = (bf16[32,512]{1,0:T(8,128)(2,1)S(1)}, bf16[32,512]{1,0:T(8,128)(2,1)S(1)}, u32[]{:S(2)}, u32[]{:S(2)}) collective-permute-start(bf16[32,512]{1,0:T(8,128)(2,1)S(1)} %get-tuple-element.734), channel_id=1, source_target_pairs={{0,16},{8,24},{16,32},{24,40},{32,48},{40,56},{48,64},{56,72},{64,... | collective-permute-start | bytes 98312 | tf_op jit(solution)/shard_map/while/body/eval_jaxpr/ppermute | solution.py:33
  667.8 4.5 collective-permute-start
  688.3 3.5 copy-start
  692.7 8.4 %collective-permute-start.1 = (bf16[32,512]{1,0:T(8,128)(2,1)S(1)}, bf16[32,512]{1,0:T(8,128)(2,1)S(1)}, u32[]{:S(2)}, u32[]{:S(2)}) collective-permute-start(bf16[32,512]{1,0:T(8,128)(2,1)S(1)} %get-tuple-element.734), channel_id=1, source_target_pairs={{0,16},{8,24},{16,32},{24,40},{32,48},{40,56},{48,64},{56,72},{64,... | collective-permute-start | bytes 98312 | tf_op jit(solution)/shard_map/while/body/eval_jaxpr/ppermute | solution.py:33
  702.0 4.4 collective-permute-start
  722.5 3.5 copy-start
  726.9 8.0 collective-permute-start.1
  735.8 4.5 collective-permute-start
  756.4 3.5 copy-start
  760.8 7.9 collective-permute-start.1
  769.6 4.5 collective-permute-start
  790.2 3.5 copy-start
  794.6 5.8 collective-permute-start.1
  800.4 0.7 copy-start.2
Sparse Core Ops, SparseCore 0:
  9.2 89.9 all-gather.4
  101.0 99.0 all-gather.6
